TPU v7x, 128 devices: a whole 4x4x4 slice. The times are simulated.
128 devices in a mesh: dp: 8 (over y, core), mp: 16 (over x, z).
Axes of the slice: x: 4, y: 4, z: 4, core: 2. Of those that a mesh axis runs over, the one named last changes fastest.
Arguments:
- emb_grad: float32 [65536, 7168], P('dp', 'mp'), may hold values from -600 to 600
- mtp_grad: float32 [14336, 7168], P('dp', 'mp'), may hold values from -600 to 600
- emb_groups: int32 [64], replicated, may hold values from 0 to 31
- mtp_groups: int32 [32], replicated, may hold values from 0 to 31
- max_rms: float32 [1], replicated, may hold values from 0.5 to 2
Outputs:
- emb_clipped: bfloat16 [65536, 7168], P(('dp', 'mp'))
- mtp_clipped: bfloat16 [14336, 7168], P('dp', 'mp')
- group_rms: float32 [32], replicated
All inputs are finite; a program needn't handle non-finite values.
Results may differ from a plain program's by a relative error of at most 0.005.
Values may be sent and summed in bfloat16 or wider, within the bound.
No kernel may reach another device: no remote copies, remote signals or barrier semaphores. Data moves between devices by JAX's collectives and lax.ppermute only.
A program may use at most 128 MiB of HBM per device.

v0:
```python
import jax
import jax.numpy as jnp
from jax import lax
from jax.sharding import Mesh
from jax.sharding import PartitionSpec as P

D = 7168
V = 65536
CAT = 14336
EMB_BLK = 1024
MTP_BLK = 448
GROUPS = 32
DP = ("dp_0", "dp_1")
DP_MP = ("dp_0", "dp_1", "mp_0", "mp_1")
MP = ("mp_0", "mp_1")


def one_axis_at_a_time(value, axes):
    for axis in axes:
        value = lax.psum(value, axis)
    return value


def block_squares(gradient, block_rows):
    blocks = gradient.reshape(gradient.shape[0] // block_rows, block_rows, gradient.shape[1])
    return jnp.sum(jnp.square(blocks), axis=(1, 2))


def membership(labels):
    return (labels[:, None] == jnp.arange(GROUPS, dtype=jnp.int32)[None, :]).astype(jnp.float32)


def on_device(emb_grad, mtp_grad, emb_groups, mtp_groups, max_rms):
    shard = lax.axis_index(DP)
    embed_count = emb_grad.shape[0] // EMB_BLK
    head_count = mtp_grad.shape[0] // MTP_BLK
    embed_labels = lax.dynamic_slice_in_dim(emb_groups, shard * embed_count, embed_count)
    head_labels = lax.dynamic_slice_in_dim(mtp_groups, shard * head_count, head_count)
    emb_low = lax.optimization_barrier(emb_grad.astype(jnp.bfloat16))
    partial_value = jnp.sum(
        block_squares(emb_grad, EMB_BLK)[:, None] * membership(embed_labels), axis=0
    )
    partial_value = partial_value + jnp.sum(
        block_squares(mtp_grad, MTP_BLK)[:, None] * membership(head_labels), axis=0
    )
    group_square = one_axis_at_a_time(partial_value, DP_MP)
    group_size = jnp.sum(membership(emb_groups), axis=0) * jnp.float32(EMB_BLK * D) + jnp.sum(
        membership(mtp_groups), axis=0
    ) * jnp.float32(MTP_BLK * D)
    group_rms = jnp.sqrt(group_square / jnp.maximum(group_size, 1.0))
    global_norm = jnp.sqrt(jnp.sum(group_square))
    ceiling = max_rms[0] * jnp.sqrt(jnp.float32((V + CAT) * D))
    factor = ceiling / (global_norm + 1e-06)
    head_output = (mtp_grad * factor).astype(jnp.bfloat16)
    scaled = (emb_low.astype(jnp.float32) * factor).astype(jnp.bfloat16)
    embed_output = lax.all_to_all(scaled, MP, split_axis=0, concat_axis=1, tiled=True)
    return (embed_output, head_output, group_rms)


def solution(mesh):
    torus = Mesh(mesh.devices.reshape(4, 2, 4, 4), ("dp_0", "dp_1", "mp_0", "mp_1"))
    return jax.shard_map(
        on_device,
        mesh=torus,
        in_specs=(P(DP, MP), P(DP, MP), P(), P(), P()),
        out_specs=(P(DP_MP, None), P(DP, MP), P()),
        check_vma=False,
    )
```

profile of v0, /device:TPU:0, one launch (start us, length us, event | category | flops | bytes accessed | tf_op | source)
XLA Modules:
  0.0 171.9 jit_solution(9425515222135174412)
XLA Ops:
  1.3 0.8 convert_reduce_fusion.1
  2.0 0.7 dynamic_slice.6
  2.8 0.7 convert_reduce_fusion
  3.5 0.7 dynamic_slice.7
  4.3 2.2 %multiply_reduce_fusion.1 = f32[1792]{0:T(1024)S(1)} fusion(f32[1792,448]{0,1:T(8,128)} %param.6), kind=kLoop, calls=%fused_computation.4 | loop fusion | flops 1603840 | bytes 3218432 | tf_op jit(solution)/shard_map/reduce_sum | solution.py:26
  6.4 0.1 reduce_sum.82
  6.5 14.2 %multiply_reduce_fusion = (f32[8192]{0:T(1024)S(1)}, bf16[8192,448]{0,1:T(8,128)(2,1)}) fusion(f32[8192,448]{0,1:T(8,128)} %param.5), kind=kLoop, calls=%fused_computation.1 | loop fusion | flops 11001856 | bytes 22052864 | tf_op jit(solution)/shard_map/reduce_sum | solution.py:26
  20.7 0.1 reduce_sum.83
  20.8 0.1 reduce_sum.79
  20.9 0.1 select_reduce_fusion.1
  21.0 0.1 select_reduce_fusion
  21.1 10.9 %psum.28 = f32[32]{0:T(128)S(1)} all-reduce(f32[32]{0:T(128)S(1)} %add.29), channel_id=1, replica_groups=mesh['dp_0'=4,'dp_1'=2,'mp_0'=4,'mp_1'=4] {'dp_0'}, use_global_device_ids=true, to_apply=%region_6.0 | all-reduce | flops 32 | bytes 256 | tf_op jit(solution)/shard_map/psum | solution.py:20
  32.0 2.5 %psum.29 = f32[32]{0:T(128)S(1)} all-reduce(f32[32]{0:T(128)S(1)} %psum.28), channel_id=1, replica_groups=mesh['dp_0'=4,'dp_1'=2,'mp_0'=4,'mp_1'=4] {'dp_1'}, use_global_device_ids=true, to_apply=%region_7.0 | all-reduce | flops 32 | bytes 256 | tf_op jit(solution)/shard_map/psum | solution.py:20
  34.4 10.5 %psum.30 = f32[32]{0:T(128)S(1)} all-reduce(f32[32]{0:T(128)S(1)} %psum.29), channel_id=1, replica_groups=mesh['dp_0'=4,'dp_1'=2,'mp_0'=4,'mp_1'=4] {'mp_0'}, use_global_device_ids=true, to_apply=%region_8.0 | all-reduce | flops 32 | bytes 256 | tf_op jit(solution)/shard_map/psum | solution.py:20
  44.9 11.8 %psum.31 = f32[32]{0:T(128)S(1)} all-reduce(f32[32]{0:T(128)S(1)} %psum.30), channel_id=1, replica_groups=mesh['dp_0'=4,'dp_1'=2,'mp_0'=4,'mp_1'=4] {'mp_1'}, use_global_device_ids=true, to_apply=%region_9.0 | all-reduce | flops 32 | bytes 256 | tf_op jit(solution)/shard_map/psum | solution.py:20
  56.6 1.1 fusion
  58.5 4.9 %multiply_convert_fusion = bf16[8192,448]{0,1:T(8,128)(2,1)S(1)} fusion(bf16[8192,448]{0,1:T(8,128)(2,1)} %get-tuple-element.16, f32[]{:T(128)S(6)} %div.6), kind=kLoop, calls=%fused_computation | loop fusion | flops 11010048 | bytes 14680068 | tf_op jit(solution)/shard_map/convert_element_type | solution.py:55
  63.4 3.9 %copy.18 = bf16[56,16,8,512]{3,2,0,1:T(8,128)(2,1)} copy(bf16[56,16,8,512]{3,2,1,0:T(8,128)(2,1)S(1)} %bitcast.9) | data formatting | bytes 14680064 | tf_op jit(solution)/shard_map/all_to_all | solution.py:56
  67.2 0.0 copy-start
  67.2 5.0 %all-to-all-start = ((bf16[16,512,448]{1,2,0:T(8,128)(2,1)}), bf16[16,512,448]{1,2,0:T(8,128)(2,1)}, u32[]{:S(2)}, u32[]{:S(2)}) async-start(bf16[16,512,448]{1,2,0:T(8,128)(2,1)} %bitcast.8), calls=%async_computation | async-start | bytes 14680064 | tf_op jit(solution)/shard_map/all_to_all | solution.py:56
  72.2 0.0 copy-done
  72.2 1.4 multiply_convert_fusion.1
  73.6 88.4 %all-to-all-done = bf16[16,512,448]{1,2,0:T(8,128)(2,1)} async-done(((bf16[16,512,448]{1,2,0:T(8,128)(2,1)}), bf16[16,512,448]{1,2,0:T(8,128)(2,1)}, u32[]{:S(2)}, u32[]{:S(2)}) %all-to-all-start) | async-done | bytes 7340064 | tf_op jit(solution)/shard_map/all_to_all | solution.py:56
  162.0 9.9 %copy.15 = bf16[512,7168]{1,0:T(8,128)(2,1)} copy(bf16[512,7168]{0,1:T(8,128)(2,1)} %bitcast.2) | data formatting | bytes 14680064
  (2 shorter events, 0.0 us)
Async XLA Ops:
  67.2 5.0 %copy-start = (f32[1792,448]{0,1:T(8,128)S(1)}, f32[1792,448]{0,1:T(8,128)}, u32[]{:S(2)}) copy-start(f32[1792,448]{0,1:T(8,128)} %param.6) | copy-start | bytes 9633796
  67.2 94.8 %all-to-all-start = ((bf16[16,512,448]{1,2,0:T(8,128)(2,1)}), bf16[16,512,448]{1,2,0:T(8,128)(2,1)}, u32[]{:S(2)}, u32[]{:S(2)}) async-start(bf16[16,512,448]{1,2,0:T(8,128)(2,1)} %bitcast.8), calls=%async_computation | async-start | bytes 14680064 | tf_op jit(solution)/shard_map/all_to_all | solution.py:56
where the time goes:
time: 173 us; the launch traced here: 172 us
  waiting for transfers between devices  88.4 us (51%)
  blocking collectives  35.5 us (21%)
  other arithmetic  25.6 us (15%)
  local copies, waits for them, and re-layouts  15.3 us (9%)
  starting transfers between devices  4.95 us (3%)
  between operations  2.06 us (1%)
    all_to_all x1, waiting for transfers between devices, on_device(): lax.all_to_all(scaled, MP, split_axis=0, concat_axis=1, tiled=True)  88.4 us
    psum x4, blocking collectives, one_axis_at_a_time(): value = lax.psum(value, axis)  35.5 us
    reduce_sum x4, other arithmetic, block_squares(): return jnp.sum(jnp.square(blocks), axis=(1, 2))  16.6 us
    unnamed x3, local copies, waits for them, and re-layouts  9.94 us
    all_to_all x1, starting transfers between devices, on_device(): lax.all_to_all(scaled, MP, split_axis=0, concat_axis=1, tiled=True)  4.95 us
    convert_element_type x1, other arithmetic, on_device(): scaled = (emb_low.astype(jnp.float32) * factor).astype(jnp.bfloat16)  4.88 us
    all_to_all x1, local copies, waits for them, and re-layouts, on_device(): lax.all_to_all(scaled, MP, split_axis=0, concat_axis=1, tiled=True)  3.85 us
  transfers between devices with their start and end apart: 1, of which 1 were waited for; matrix products, arithmetic and copies ran while one was open for 1% of the time, Pallas kernels for 0%

commit v1 on v0

--- a/solution.py
+++ b/solution.py
@@ -15,9 +15,15 @@
 MP = ("mp_0", "mp_1")
 
 
+def add_all(x, mesh_axis):
+    parts = lax.all_gather(x, mesh_axis, axis=0, tiled=False)
+    summed = parts.sum(axis=0)
+    return summed
+
+
 def one_axis_at_a_time(value, axes):
     for axis in axes:
-        value = lax.psum(value, axis)
+        value = add_all(value, axis)
     return value
 
 

time: 173 us -> 178 us (1.029)
  local copies, waits for them, and re-layouts: 15.3 us -> 20.1 us
  between operations: 2.06 us -> 4.67 us
    psum x4 -> x0, blocking collectives: 35.5 us -> none  [one_axis_at_a_time(): value = lax.psum(value, axis)]
    unnamed x0 -> x4, blocking collectives: none -> 35.5 us
    unnamed x3 -> x18, local copies, waits for them, and re-layouts: 9.94 us -> 15.6 us
where the time goes in v1:
time: 178 us; the launch traced here: 177 us
  waiting for transfers between devices  87.6 us (49%)
  blocking collectives  35.5 us (20%)
  other arithmetic  24.5 us (14%)
  local copies, waits for them, and re-layouts  20.1 us (11%)
  starting transfers between devices  4.95 us (3%)
  between operations  4.67 us (3%)
    all_to_all x1, waiting for transfers between devices, on_device(): lax.all_to_all(scaled, MP, split_axis=0, concat_axis=1, tiled=True)  87.6 us
    unnamed x4, blocking collectives  35.5 us
    reduce_sum x4, other arithmetic, block_squares(): return jnp.sum(jnp.square(blocks), axis=(1, 2))  16.6 us
    unnamed x18, local copies, waits for them, and re-layouts  15.6 us
    all_to_all x1, starting transfers between devices, on_device(): lax.all_to_all(scaled, MP, split_axis=0, concat_axis=1, tiled=True)  4.95 us
    convert_element_type x1, other arithmetic, on_device(): scaled = (emb_low.astype(jnp.float32) * factor).astype(jnp.bfloat16)  4.88 us
    all_to_all x1, local copies, waits for them, and re-layouts, on_device(): lax.all_to_all(scaled, MP, split_axis=0, concat_axis=1, tiled=True)  3.85 us
  transfers between devices with their start and end apart: 1, of which 1 were waited for; matrix products, arithmetic and copies ran while one was open for 1% of the time, Pallas kernels for 0%

profile of v1, /device:TPU:0, one launch (start us, length us, event | category | flops | bytes accessed | tf_op | source)
XLA Modules:
  0.0 177.3 jit_solution(16916008249992952427)
XLA Ops:
  1.3 1.2 dynamic-slice.3
  2.5 1.2 dynamic-slice.2
  5.1 1.2 dynamic-slice.1
  7.0 1.2 dynamic-slice
  8.9 2.2 %multiply_reduce_fusion.1 = f32[1792]{0:T(1024)S(1)} fusion(f32[1792,448]{0,1:T(8,128)} %param.6), kind=kLoop, calls=%fused_computation.4 | loop fusion | flops 1603840 | bytes 3218432 | tf_op jit(solution)/shard_map/reduce_sum | solution.py:32
  11.1 14.2 %multiply_reduce_fusion = (f32[8192]{0:T(1024)S(1)}, bf16[8192,448]{0,1:T(8,128)(2,1)}) fusion(f32[8192,448]{0,1:T(8,128)} %param.5), kind=kLoop, calls=%fused_computation.1 | loop fusion | flops 11001856 | bytes 22052864 | tf_op jit(solution)/shard_map/reduce_sum | solution.py:32
  25.5 0.1 reduce_sum.119
  25.6 0.1 select_reduce_fusion.1
  25.7 0.1 reduce_sum.115
  25.8 0.1 select_reduce_fusion
  25.9 0.1 add_dynamic-update-slice_fusion
  26.0 10.8 %all-reduce = f32[128]{0:T(128)S(1)} all-reduce(f32[128]{0:T(128)S(1)} %add_dynamic-update-slice_fusion), channel_id=2, replica_groups=mesh['dp_0'=4,'dp_1'=2,'mp_0'=4,'mp_1'=4] {'dp_0'}, use_global_device_ids=true, to_apply=%add | all-reduce | flops 128 | bytes 1024
  36.8 0.1 reshape.33
  36.9 0.2 dynamic-update-slice.1
  37.2 2.4 %all-reduce.1 = f32[64]{0:T(128)S(1)} all-reduce(f32[64]{0:T(128)S(1)} %dynamic-update-slice.1), channel_id=3, replica_groups=mesh['dp_0'=4,'dp_1'=2,'mp_0'=4,'mp_1'=4] {'dp_1'}, use_global_device_ids=true, to_apply=%add.1 | all-reduce | flops 64 | bytes 512
  39.6 0.1 reshape.34
  39.7 0.2 dynamic-update-slice.2
  40.0 10.5 %all-reduce.2 = f32[128]{0:T(128)S(1)} all-reduce(f32[128]{0:T(128)S(1)} %dynamic-update-slice.2), channel_id=4, replica_groups=mesh['dp_0'=4,'dp_1'=2,'mp_0'=4,'mp_1'=4] {'mp_0'}, use_global_device_ids=true, to_apply=%add.2 | all-reduce | flops 128 | bytes 1024
  50.4 0.1 reshape.35
  50.5 0.2 dynamic-update-slice.3
  50.8 11.7 %all-reduce.3 = f32[128]{0:T(128)S(1)} all-reduce(f32[128]{0:T(128)S(1)} %dynamic-update-slice.3), channel_id=5, replica_groups=mesh['dp_0'=4,'dp_1'=2,'mp_0'=4,'mp_1'=4] {'mp_1'}, use_global_device_ids=true, to_apply=%add.3 | all-reduce | flops 128 | bytes 1024
  62.5 0.6 reduce_sum.124
  63.9 4.9 %multiply_convert_fusion = bf16[8192,448]{0,1:T(8,128)(2,1)S(1)} fusion(bf16[8192,448]{0,1:T(8,128)(2,1)} %get-tuple-element.16, f32[]{:T(128)S(6)} %div.6), kind=kLoop, calls=%fused_computation | loop fusion | flops 11010048 | bytes 14680068 | tf_op jit(solution)/shard_map/convert_element_type | solution.py:61
  68.8 3.9 %copy.18 = bf16[56,16,8,512]{3,2,0,1:T(8,128)(2,1)} copy(bf16[56,16,8,512]{3,2,1,0:T(8,128)(2,1)S(1)} %bitcast.13) | data formatting | bytes 14680064 | tf_op jit(solution)/shard_map/all_to_all | solution.py:62
  72.6 5.0 %all-to-all-start = ((bf16[16,512,448]{1,2,0:T(8,128)(2,1)}), bf16[16,512,448]{1,2,0:T(8,128)(2,1)}, u32[]{:S(2)}, u32[]{:S(2)}) async-start(bf16[16,512,448]{1,2,0:T(8,128)(2,1)} %bitcast.12), calls=%async_computation | async-start | bytes 14680064 | tf_op jit(solution)/shard_map/all_to_all | solution.py:62
  77.6 0.1 reshape.36
  77.7 0.1 convert_reduce_fusion.1
  77.8 0.1 convert_reduce_fusion
  77.9 0.5 fusion
  78.4 1.4 multiply_convert_fusion.1
  79.8 87.6 %all-to-all-done = bf16[16,512,448]{1,2,0:T(8,128)(2,1)} async-done(((bf16[16,512,448]{1,2,0:T(8,128)(2,1)}), bf16[16,512,448]{1,2,0:T(8,128)(2,1)}, u32[]{:S(2)}, u32[]{:S(2)}) %all-to-all-start) | async-done | bytes 7340064 | tf_op jit(solution)/shard_map/all_to_all | solution.py:62
  167.4 9.9 %copy.15 = bf16[512,7168]{1,0:T(8,128)(2,1)} copy(bf16[512,7168]{0,1:T(8,128)(2,1)} %bitcast.6) | data formatting | bytes 14680064
  (18 shorter events, 0.4 us)
Async XLA Ops:
  11.1 14.2 %copy-start.1 = (s32[64]{0:T(128)S(1)}, s32[64]{0:T(128)}, u32[]{:S(2)}) copy-start(s32[64]{0:T(128)} %param.7) | copy-start | bytes 772
  11.1 14.3 %copy-start.2 = (s32[32]{0:T(128)S(1)}, s32[32]{0:T(128)}, u32[]{:S(2)}) copy-start(s32[32]{0:T(128)} %param.8) | copy-start | bytes 388
  72.6 5.8 %copy-start = (f32[1792,448]{0,1:T(8,128)S(1)}, f32[1792,448]{0,1:T(8,128)}, u32[]{:S(2)}) copy-start(f32[1792,448]{0,1:T(8,128)} %param.6) | copy-start | bytes 9633796
  72.6 94.8 %all-to-all-start = ((bf16[16,512,448]{1,2,0:T(8,128)(2,1)}), bf16[16,512,448]{1,2,0:T(8,128)(2,1)}, u32[]{:S(2)}, u32[]{:S(2)}) async-start(bf16[16,512,448]{1,2,0:T(8,128)(2,1)} %bitcast.12), calls=%async_computation | async-start | bytes 14680064 | tf_op jit(solution)/shard_map/all_to_all | solution.py:62
